TPU v7x, 32 devices: a whole 2x2x4 slice. The times are simulated.
32 devices in a mesh: head: 4 (over y, core), seq: 8 (over z, x).
Axes of the slice: x: 2, y: 2, z: 4, core: 2. Of those that a mesh axis runs over, the one named last changes fastest.
Arguments:
- queries: bfloat16 [8192, 4096], P('seq', 'head'), may hold values from -6 to 6
- keys: bfloat16 [8192, 512], P('seq', 'head'), may hold values from -6 to 6
- values: bfloat16 [8192, 512], P('seq', 'head'), may hold values from -6 to 6
- vertical: int32 [32, 8], P('head'), may hold values from 0 to 63, as said below
- slash: int32 [32, 8], P('head'), may hold values from 1 to 28, as said below
Outputs:
- attended: bfloat16 [8192, 4096], P(('seq', 'head'))
Inputs may be any that keep to these rules, and one draw needn't show every extreme that they name: `vertical`: each row names 8 different blocks. Within each group of 8 consecutive rows, the different blocks named that lie in one slab (blocks s * 8 to s * 8 + 7) number at most 4, and exactly 4 in some slab. `slash`: each row names 8 different offsets.
All inputs are finite; a program needn't handle non-finite values.
Results may differ from a plain program's by a relative error of at most 0.0033.
Values may be sent and summed in bfloat16 or wider, within the bound.
A program may use at most 128 MiB of HBM per device.

v0:
```python
import math

import jax
import jax.numpy as jnp
from jax import lax
from jax.sharding import PartitionSpec as P

BLK = 128
LARGEST_OFFSET = 28
CAP = 4


NEG = -1e30


def shifted(array, axis, by):
    peers = lax.axis_size(axis)
    pairs = [(i, i + by) for i in range(peers) if 0 <= i + by < peers]
    return lax.ppermute(array, axis, pairs)


def attend(query_block, diag_kv, slash_parts, column_kv, slash_ok, column_ok):
    block_count, block_width, head_width = query_block.shape
    score_scale = 1.0 / math.sqrt(head_width)
    causal = jnp.arange(block_width)[:, None] >= jnp.arange(block_width)[None, :]
    diag_scores = (
        jnp.einsum(
            "ird,icd->irc",
            query_block,
            diag_kv[..., :head_width],
            preferred_element_type=jnp.float32,
        )
        * score_scale
    )
    diag_scores = jnp.where(causal[None], diag_scores, NEG)
    slash_scores = []
    for number, part_kv in enumerate(slash_parts):
        part_scores = (
            jnp.einsum(
                "ird,icd->irc",
                query_block,
                part_kv[..., :head_width],
                preferred_element_type=jnp.float32,
            )
            * score_scale
        )
        slash_scores.append(jnp.where(slash_ok[:, number, None, None], part_scores, NEG))
    column_scores = (
        jnp.einsum(
            "ird,jcd->irjc",
            query_block,
            column_kv[..., :head_width],
            preferred_element_type=jnp.float32,
        )
        * score_scale
    )
    column_scores = jnp.where(column_ok[:, None, :, None], column_scores, NEG)
    row_top = jnp.maximum(jnp.max(diag_scores, axis=2), jnp.max(column_scores, axis=(2, 3)))
    for part_scores in slash_scores:
        row_top = jnp.maximum(row_top, jnp.max(part_scores, axis=2))
    diag_weights = jnp.exp(diag_scores - row_top[:, :, None])
    column_weights = jnp.exp(column_scores - row_top[:, :, None, None])
    row_total = jnp.sum(diag_weights, axis=2) + jnp.sum(column_weights, axis=(2, 3))
    mixed_sum = jnp.einsum(
        "irc,icd->ird",
        diag_weights.astype(jnp.bfloat16),
        diag_kv[..., head_width:],
        preferred_element_type=jnp.float32,
    )
    mixed_sum = mixed_sum + jnp.einsum(
        "irjc,jcd->ird",
        column_weights.astype(jnp.bfloat16),
        column_kv[..., head_width:],
        preferred_element_type=jnp.float32,
    )
    for part_scores, part_kv in zip(slash_scores, slash_parts):
        part_weights = jnp.exp(part_scores - row_top[:, :, None])
        row_total = row_total + jnp.sum(part_weights, axis=2)
        mixed_sum = mixed_sum + jnp.einsum(
            "irc,icd->ird",
            part_weights.astype(jnp.bfloat16),
            part_kv[..., head_width:],
            preferred_element_type=jnp.float32,
        )
    return (mixed_sum / row_total[:, :, None]).astype(jnp.bfloat16)


def shards(queries, keys, values, vertical, slash):
    head_width = keys.shape[1]
    slab_rows = queries.shape[0]
    slab_blocks = slab_rows // BLK
    group_heads = vertical.shape[0]
    column_count = vertical.shape[1]
    slash_count = slash.shape[1]
    reach = (LARGEST_OFFSET + slab_blocks - 1) // slab_blocks
    slab_index = lax.axis_index("seq")
    local_kv = jnp.concatenate([keys, values], axis=1)
    flat_columns = vertical.reshape(-1)
    block_ids = slab_index * slab_blocks + jnp.arange(slab_blocks, dtype=jnp.int32)
    used = jnp.any(flat_columns[:, None] == block_ids[None, :], axis=0)
    ranks = jnp.cumsum(used.astype(jnp.int32)) - 1
    select = used[None, :] & (ranks[None, :] == jnp.arange(CAP, dtype=jnp.int32)[:, None])
    packed = jnp.dot(
        select.astype(jnp.bfloat16),
        local_kv.reshape(slab_blocks, BLK * 2 * head_width),
        preferred_element_type=jnp.float32,
    )
    packed = packed.astype(jnp.bfloat16).reshape(CAP, BLK, 2 * head_width)
    packed_ids = jnp.where(
        jnp.any(select, axis=1), jnp.sum(jnp.where(select, block_ids[None, :], 0), axis=1), -1
    )
    all_packed, all_ids = (
        lax.all_gather(packed, "seq", axis=0, tiled=True),
        lax.all_gather(packed_ids, "seq", axis=0, tiled=True),
    )
    slot_ids = jnp.arange(all_ids.shape[0], dtype=jnp.int32)
    position = jnp.sum(
        jnp.where(all_ids[None, :] == flat_columns[:, None], slot_ids[None, :], 0), axis=1
    )
    column_kv = jnp.take(all_packed, position, axis=0).reshape(
        group_heads, column_count, BLK, 2 * head_width
    )
    earlier_parts = [local_kv]
    moving = local_kv
    for step_back in range(reach):
        moving = shifted(moving, "seq", 1)
        earlier_parts = [moving] + earlier_parts
    extended = jnp.concatenate(earlier_parts, axis=0)
    extended_blocks = extended.reshape(-1, BLK, 2 * head_width)
    base_block = reach * slab_blocks
    diag_kv = extended_blocks[base_block : base_block + slab_blocks]
    local_ids = jnp.arange(slab_blocks, dtype=jnp.int32)
    global_ids = slab_index * slab_blocks + local_ids

    def one_head(head_index, attended):
        query_block = lax.dynamic_slice_in_dim(
            queries, head_index * head_width, head_width, 1
        ).reshape(slab_blocks, BLK, head_width)
        offsets = lax.dynamic_index_in_dim(slash, head_index, 0, keepdims=False)
        columns = lax.dynamic_index_in_dim(vertical, head_index, 0, keepdims=False)
        head_kv = lax.dynamic_index_in_dim(column_kv, head_index, 0, keepdims=False)
        slash_parts = [
            lax.dynamic_slice_in_dim(extended_blocks, base_block - offsets[number], slab_blocks, 0)
            for number in range(slash_count)
        ]
        slash_ok = global_ids[:, None] - offsets[None, :] >= 0
        covered = jnp.any(
            global_ids[:, None, None] - columns[None, :, None] == offsets[None, None, :], axis=2
        )
        column_ok = (columns[None, :] < global_ids[:, None]) & jnp.logical_not(covered)
        result = attend(query_block, diag_kv, slash_parts, head_kv, slash_ok, column_ok)
        return lax.dynamic_update_slice_in_dim(
            attended, result.reshape(slab_rows, head_width), head_index * head_width, 1
        )

    attended = lax.fori_loop(
        0, group_heads, one_head, jnp.zeros((slab_rows, group_heads * head_width), jnp.bfloat16)
    )
    return lax.all_to_all(attended, "head", split_axis=0, concat_axis=1, tiled=True)


def solution(mesh):
    in_specs = (
        P("seq", "head"),
        P("seq", "head"),
        P("seq", "head"),
        P("head", None),
        P("head", None),
    )
    out_specs = P(("seq", "head"), None)
    return jax.shard_map(shards, mesh=mesh, in_specs=in_specs, out_specs=out_specs, check_vma=False)
```

profile of v0, /device:TPU:27, one launch (start us, length us, event | category | flops | bytes accessed | tf_op | source)
XLA Modules:
  0.0 551.1 jit_solution(8465910710655638386)
XLA Ops:
  14.9 16.5 %collective-permute-done = bf16[1024,256]{1,0:T(8,128)(2,1)S(1)} collective-permute-done((bf16[1024,256]{1,0:T(8,128)(2,1)}, bf16[1024,256]{1,0:T(8,128)(2,1)S(1)}, u32[]{:S(2)}, u32[]{:S(2)}) %collective-permute-start) | collective-permute-done | bytes 524320 | tf_op jit(solution)/shard_map/ppermute | solution.py:19
  33.9 16.4 %collective-permute-done.1 = bf16[1024,256]{1,0:T(8,128)(2,1)S(1)} collective-permute-done((bf16[1024,256]{1,0:T(8,128)(2,1)S(1)}, bf16[1024,256]{1,0:T(8,128)(2,1)S(1)}, u32[]{:S(2)}, u32[]{:S(2)}) %collective-permute-start.1) | collective-permute-done | bytes 524320 | tf_op jit(solution)/shard_map/ppermute | solution.py:19
  52.0 25.6 %all-reduce = s32[32]{0:T(128)S(1)} all-reduce(s32[32]{0:T(128)S(1)} %select_dynamic-update-slice_fusion), channel_id=1, replica_groups=mesh['head'=4,'seq'=8] {'seq'}, use_global_device_ids=true, to_apply=%add | all-reduce | flops 32 | bytes 256
  79.1 9.3 %collective-permute-done.3 = bf16[1024,256]{1,0:T(8,128)(2,1)S(1)} collective-permute-done((bf16[1024,256]{1,0:T(8,128)(2,1)S(1)}, bf16[1024,256]{1,0:T(8,128)(2,1)S(1)}, u32[]{:S(2)}, u32[]{:S(2)}) %collective-permute-start.3) | collective-permute-done | bytes 524320 | tf_op jit(solution)/shard_map/ppermute | solution.py:19
  91.0 5.3 gather_fusion
  96.3 4.6 broadcast_select_fusion
  102.4 401.5 %while.17 = (s32[]{:T(128)}, bf16[1024,1024]{1,0:T(8,128)(2,1)}, bf16[1024,1024]{1,0:T(8,128)(2,1)}, bf16[8,128,256]{2,1,0:T(8,128)(2,1)}, s32[8,8]{1,0:T(8,128)...) while((s32[]{:T(128)}, bf16[1024,1024]{1,0:T(8,128)(2,1)}, ...), condition=%wide.region_27.28_spmd.clone, body=%wide.region_5.27_spmd.clone.sunk | while | flops 1162099968 | bytes 94896152 | solution.py:156
  107.1 2.7 fusion.199
  124.0 2.1 fusion.205
  137.4 3.9 fusion.210
  157.3 2.7 fusion.199
  174.2 2.1 fusion.205
  187.6 3.9 fusion.210
  207.5 2.7 fusion.199
  224.4 2.1 fusion.205
  237.8 3.9 fusion.210
  257.7 2.7 fusion.199
  274.6 2.1 fusion.205
  288.0 3.9 fusion.210
  307.9 2.7 fusion.199
  324.8 2.1 fusion.205
  338.2 3.9 fusion.210
  358.1 2.7 fusion.199
  375.0 2.1 fusion.205
  388.4 3.9 fusion.210
  408.3 2.7 fusion.199
  438.6 3.9 fusion.210
  458.5 2.7 fusion.199
  488.8 3.9 fusion.210
  503.9 33.7 %all_to_all.19 = bf16[4,256,1024]{2,1,0:T(8,128)(2,1)S(1)} all-to-all(bf16[4,256,1024]{2,1,0:T(8,128)(2,1)} %bitcast.152), channel_id=1, replica_groups=mesh['head'=4,'seq'=8] {'head'}, dimensions={0} | all-to-all | bytes 4194304 | tf_op jit(solution)/shard_map/all_to_all | solution.py:159
  537.6 2.6 copy.67
  540.2 4.1 copy.68
  (518 shorter events, 273.1 us)
Async XLA Ops:
  6.5 26.1 %copy-start.19 = (u32[32]{0:T(128)S(1)}, u32[32]{0:T(128)}, u32[]{:S(2)}) copy-start(u32[32]{0:T(128)} %constant.198) | copy-start | bytes 388
  6.5 84.4 %all-gather.2.cloned.1.call-start = ((), (), s32[]{:S(2)}) async-start(), calls=%async_computation.1 | async-start | bytes 2359296 | tf_op jit(solution)/shard_map/all_gather | solution.py:113
  12.6 78.1 %copy-start.13 = (bf16[1024,128]{1,0:T(8,128)(2,1)S(1)}, bf16[1024,128]{1,0:T(8,128)(2,1)}, u32[]{:S(2)}) copy-start(bf16[1024,128]{1,0:T(8,128)(2,1)} %param.8) | copy-start | bytes 786436
  13.4 77.5 %copy-start.14 = (bf16[1024,128]{1,0:T(8,128)(2,1)S(1)}, bf16[1024,128]{1,0:T(8,128)(2,1)}, u32[]{:S(2)}) copy-start(bf16[1024,128]{1,0:T(8,128)(2,1)} %param.9) | copy-start | bytes 786436
  13.4 18.0 %collective-permute-start = (bf16[1024,256]{1,0:T(8,128)(2,1)}, bf16[1024,256]{1,0:T(8,128)(2,1)S(1)}, u32[]{:S(2)}, u32[]{:S(2)}) collective-permute-start(bf16[1024,256]{1,0:T(8,128)(2,1)} %constant_dynamic-update-slice_fusion.1), channel_id=1, source_target_pairs={{0,1},{1,2},{2,3},{3,4},{4,5},{5,6},{6,7},{8,9},{9,10},{10,11},{11... | collective-permute-start | bytes 1572872 | tf_op jit(solution)/shard_map/ppermute | solution.py:19
  31.4 47.7 %copy-start.15 = (bf16[1024,256]{1,0:T(8,128)(2,1)}, bf16[1024,256]{1,0:T(8,128)(2,1)S(1)}, u32[]{:S(2)}) copy-start(bf16[1024,256]{1,0:T(8,128)(2,1)S(1)} %collective-permute-done) | copy-start | bytes 1572868
  31.4 19.0 %collective-permute-start.1 = (bf16[1024,256]{1,0:T(8,128)(2,1)S(1)}, bf16[1024,256]{1,0:T(8,128)(2,1)S(1)}, u32[]{:S(2)}, u32[]{:S(2)}) collective-permute-start(bf16[1024,256]{1,0:T(8,128)(2,1)S(1)} %collective-permute-done), channel_id=1, source_target_pairs={{0,1},{1,2},{2,3},{3,4},{4,5},{5,6},{6,7},{8,9},{9,10},{10,11},{11... | collective-permute-start | bytes 1572872 | tf_op jit(solution)/shard_map/ppermute | solution.py:19
  50.3 28.7 %copy-start.17 = (bf16[1024,256]{1,0:T(8,128)(2,1)}, bf16[1024,256]{1,0:T(8,128)(2,1)S(1)}, u32[]{:S(2)}) copy-start(bf16[1024,256]{1,0:T(8,128)(2,1)S(1)} %collective-permute-done.1) | copy-start | bytes 1572868
  50.3 27.4 %collective-permute-start.2 = (bf16[1024,256]{1,0:T(8,128)(2,1)S(1)}, bf16[1024,256]{1,0:T(8,128)(2,1)S(1)}, u32[]{:S(2)}, u32[]{:S(2)}) collective-permute-start(bf16[1024,256]{1,0:T(8,128)(2,1)S(1)} %collective-permute-done.1), channel_id=1, source_target_pairs={{0,1},{1,2},{2,3},{3,4},{4,5},{5,6},{6,7},{8,9},{9,10},{10,11},{11... | collective-permute-start | bytes 1572872 | tf_op jit(solution)/shard_map/ppermute | solution.py:19
  77.7 10.7 %collective-permute-start.3 = (bf16[1024,256]{1,0:T(8,128)(2,1)S(1)}, bf16[1024,256]{1,0:T(8,128)(2,1)S(1)}, u32[]{:S(2)}, u32[]{:S(2)}) collective-permute-start(bf16[1024,256]{1,0:T(8,128)(2,1)S(1)} %collective-permute-done.2), channel_id=1, source_target_pairs={{0,1},{1,2},{2,3},{3,4},{4,5},{5,6},{6,7},{8,9},{9,10},{10,11},{11... | collective-permute-start | bytes 1572872 | tf_op jit(solution)/shard_map/ppermute | solution.py:19
  90.9 5.3 copy-start.1
  107.1 5.6 %copy-start.2 = (bf16[40,128,256]{2,1,0:T(8,128)(2,1)S(1)}, bf16[40,128,256]{2,1,0:T(8,128)(2,1)}, u32[]{:S(2)}) copy-start(bf16[40,128,256]{2,1,0:T(8,128)(2,1)} %get-tuple-element.530) | copy-start | bytes 7864324 | tf_op jit(solution)/shard_map/while
  137.4 3.9 copy-start.10
  143.4 3.3 copy-start.5
  157.3 5.6 %copy-start.2 = (bf16[40,128,256]{2,1,0:T(8,128)(2,1)S(1)}, bf16[40,128,256]{2,1,0:T(8,128)(2,1)}, u32[]{:S(2)}) copy-start(bf16[40,128,256]{2,1,0:T(8,128)(2,1)} %get-tuple-element.530) | copy-start | bytes 7864324 | tf_op jit(solution)/shard_map/while
  187.6 3.9 copy-start.10
  193.6 3.3 copy-start.5
  207.5 5.6 %copy-start.2 = (bf16[40,128,256]{2,1,0:T(8,128)(2,1)S(1)}, bf16[40,128,256]{2,1,0:T(8,128)(2,1)}, u32[]{:S(2)}) copy-start(bf16[40,128,256]{2,1,0:T(8,128)(2,1)} %get-tuple-element.530) | copy-start | bytes 7864324 | tf_op jit(solution)/shard_map/while
  237.8 3.9 copy-start.10
  243.8 3.3 copy-start.5
  257.7 5.6 %copy-start.2 = (bf16[40,128,256]{2,1,0:T(8,128)(2,1)S(1)}, bf16[40,128,256]{2,1,0:T(8,128)(2,1)}, u32[]{:S(2)}) copy-start(bf16[40,128,256]{2,1,0:T(8,128)(2,1)} %get-tuple-element.530) | copy-start | bytes 7864324 | tf_op jit(solution)/shard_map/while
  288.0 3.9 copy-start.10
  294.0 3.3 copy-start.5
  307.9 5.6 %copy-start.2 = (bf16[40,128,256]{2,1,0:T(8,128)(2,1)S(1)}, bf16[40,128,256]{2,1,0:T(8,128)(2,1)}, u32[]{:S(2)}) copy-start(bf16[40,128,256]{2,1,0:T(8,128)(2,1)} %get-tuple-element.530) | copy-start | bytes 7864324 | tf_op jit(solution)/shard_map/while
  338.2 3.9 copy-start.10
  344.2 3.3 copy-start.5
  358.1 5.6 %copy-start.2 = (bf16[40,128,256]{2,1,0:T(8,128)(2,1)S(1)}, bf16[40,128,256]{2,1,0:T(8,128)(2,1)}, u32[]{:S(2)}) copy-start(bf16[40,128,256]{2,1,0:T(8,128)(2,1)} %get-tuple-element.530) | copy-start | bytes 7864324 | tf_op jit(solution)/shard_map/while
  388.3 3.9 copy-start.10
  408.3 5.6 %copy-start.2 = (bf16[40,128,256]{2,1,0:T(8,128)(2,1)S(1)}, bf16[40,128,256]{2,1,0:T(8,128)(2,1)}, u32[]{:S(2)}) copy-start(bf16[40,128,256]{2,1,0:T(8,128)(2,1)} %get-tuple-element.530) | copy-start | bytes 7864324 | tf_op jit(solution)/shard_map/while
  438.5 3.9 copy-start.10
  458.5 5.6 %copy-start.2 = (bf16[40,128,256]{2,1,0:T(8,128)(2,1)S(1)}, bf16[40,128,256]{2,1,0:T(8,128)(2,1)}, u32[]{:S(2)}) copy-start(bf16[40,128,256]{2,1,0:T(8,128)(2,1)} %get-tuple-element.530) | copy-start | bytes 7864324 | tf_op jit(solution)/shard_map/while
  488.7 3.9 copy-start.10
  (77 other events, 129.1 us)
Sparse Core Ops, SparseCore 0:
  13.5 58.1 all-gather.1
where the time goes:
time: 560 us; the launch traced here: 551 us
  matrix products  236 us (42%)
  local copies, waits for them, and re-layouts  85.5 us (15%)
  loops' own time  80.4 us (14%)
  blocking collectives  59.3 us (11%)
  waiting for transfers between devices  42.3 us (8%)
  other arithmetic  27.9 us (5%)
  between operations  14.2 us (3%)
    dot_general x64, matrix products, attend(): jnp.einsum('ird,icd->irc', query_block, part_kv[..., :head_width], prefer...  118 us
    another operation x1, loops' own time, shards(): lax.fori_loop(0, group_heads, one_head, jnp.zeros((slab_rows, group_heads...  80.4 us
    ppermute x4, waiting for transfers between devices, shifted(): return lax.ppermute(array, axis, pairs)  42.3 us
    dot_general x64, matrix products, attend(): jnp.einsum('irc,icd->ird', part_weights.astype(jnp.bfloat16), part_kv[......  38.4 us
    all_to_all x1, blocking collectives, shards(): lax.all_to_all(attended, 'head', split_axis=0, concat_axis=1, tiled=True)  33.7 us
    dot_general x8, matrix products, attend(): jnp.einsum('irjc,jcd->ird', column_weights.astype(jnp.bfloat16), column_k...  31.2 us
    unnamed x1, blocking collectives  25.6 us
    dot_general x8, matrix products, attend(): jnp.einsum('ird,jcd->irjc', query_block, column_kv[..., :head_width], pre...  21.5 us
  transfers between devices with their start and end apart: 5, of which 3 were waited for; matrix products, arithmetic and copies ran while one was open for 1% of the time, Pallas kernels for 0%

commit v1 on v0

v1 whole, which is shorter than its diff:
```python
import functools
import math

import jax
import jax.numpy as jnp
from jax import lax
from jax.experimental import pallas as pl
from jax.experimental.pallas import tpu as pltpu
from jax.sharding import PartitionSpec as P

BLK = 128
NEG = -1e30


def attention_kernel(slab_ref, index_ref, bias_ref, q_ref, kt_ref, v_ref, out_ref, *, blocks, listed, width):
    head = pl.program_id(0)
    base = slab_ref[0] * blocks
    factor = math.log2(math.e) / math.sqrt(width)
    causal = lax.broadcasted_iota(jnp.int32, (BLK, BLK), 0) >= lax.broadcasted_iota(
        jnp.int32, (BLK, BLK), 1
    )

    def one_block(i, carry):
        rows = pl.ds(pl.multiple_of(i * BLK, BLK), BLK)
        q = q_ref[rows, :]
        row = (head * blocks + i) * listed
        own = base + i
        scores = [
            jnp.where(causal, jnp.dot(q, kt_ref[own], preferred_element_type=jnp.float32), NEG)
        ]
        for n in range(0, listed, 2):
            a, b = index_ref[row + n], index_ref[row + n + 1]
            pair = jnp.dot(
                q, jnp.concatenate([kt_ref[a], kt_ref[b]], axis=1), preferred_element_type=jnp.float32
            )
            scores.append(pair[:, :BLK] + bias_ref[row + n])
            scores.append(pair[:, BLK:] + bias_ref[row + n + 1])
        top = functools.reduce(jnp.maximum, scores)
        top = jnp.max(top, axis=1, keepdims=True) * factor
        total = None
        rounded = []
        for s in scores:
            w = jnp.exp2(s * factor - top)
            total = w if total is None else total + w
            rounded.append(w.astype(jnp.bfloat16))
        mixed = jnp.dot(rounded[0], v_ref[own], preferred_element_type=jnp.float32)
        for n in range(0, listed, 2):
            a, b = index_ref[row + n], index_ref[row + n + 1]
            mixed += jnp.dot(
                jnp.concatenate([rounded[1 + n], rounded[2 + n]], axis=1),
                jnp.concatenate([v_ref[a], v_ref[b]], axis=0),
                preferred_element_type=jnp.float32,
            )
        total = jnp.sum(total, axis=1, keepdims=True)
        out_ref[rows, :] = (mixed / total).astype(jnp.bfloat16)
        return carry

    lax.fori_loop(0, blocks, one_block, 0, unroll=2)


def block_lists(vertical, slash, slab_index, blocks):
    ids = slab_index * blocks + jnp.arange(blocks, dtype=jnp.int32)
    slash_ids = ids[None, :, None] - slash[:, None, :]
    slash_ok = slash_ids >= 0
    columns = jnp.broadcast_to(vertical[:, None, :], slash_ids.shape[:2] + vertical.shape[1:])
    covered = jnp.any(columns[..., None] == slash_ids[:, :, None, :], axis=3)
    column_ok = (columns < ids[None, :, None]) & jnp.logical_not(covered)
    listed = jnp.concatenate([slash_ids, columns], axis=2)
    ok = jnp.concatenate([slash_ok, column_ok], axis=2)
    index = jnp.where(ok, listed, ids[None, :, None])
    bias = jnp.where(ok, 0.0, NEG).astype(jnp.float32)
    return index.reshape(-1), bias.reshape(-1), listed.shape[2]


def shards(queries, keys, values, vertical, slash):
    width = keys.shape[1]
    rows = queries.shape[0]
    blocks = rows // BLK
    heads = vertical.shape[0]
    slab_index = lax.axis_index("seq")
    kt = jnp.swapaxes(keys.reshape(blocks, BLK, width), 1, 2)
    v = values.reshape(blocks, BLK, width)
    index, bias, listed = block_lists(vertical, slash, slab_index, blocks)
    kt_all = lax.all_gather(kt, "seq", axis=0, tiled=True)
    v_all = lax.all_gather(v, "seq", axis=0, tiled=True)
    attended = pl.pallas_call(
        functools.partial(attention_kernel, blocks=blocks, listed=listed, width=width),
        grid_spec=pltpu.PrefetchScalarGridSpec(
            num_scalar_prefetch=3,
            grid=(heads,),
            in_specs=[
                pl.BlockSpec((rows, width), lambda h, *_: (0, h)),
                pl.BlockSpec(memory_space=pltpu.VMEM),
                pl.BlockSpec(memory_space=pltpu.VMEM),
            ],
            out_specs=pl.BlockSpec((rows, width), lambda h, *_: (0, h)),
        ),
        out_shape=jax.ShapeDtypeStruct((rows, heads * width), jnp.bfloat16),
        compiler_params=pltpu.CompilerParams(
            dimension_semantics=("arbitrary",), vmem_limit_bytes=60 * 1024 * 1024
        ),
    )(slab_index.reshape(1).astype(jnp.int32), index, bias, queries, kt_all, v_all)
    return lax.all_to_all(attended, "head", split_axis=0, concat_axis=1, tiled=True)


def solution(mesh):
    in_specs = (
        P("seq", "head"),
        P("seq", "head"),
        P("seq", "head"),
        P("head", None),
        P("head", None),
    )
    out_specs = P(("seq", "head"), None)
    return jax.shard_map(shards, mesh=mesh, in_specs=in_specs, out_specs=out_specs, check_vma=False)
```

time: 560 us -> 197 us (0.35)
  the two profiles are of different devices: /device:TPU:27 before, /device:TPU:0 now
where the time goes in v1:
time: 197 us
  waiting for transfers between devices  97 us (49%)
  Pallas kernels  47.9 us (24%)
  blocking collectives  29.2 us (15%)
  between operations  13.4 us (7%)
  local copies, waits for them, and re-layouts  5.31 us (3%)
  other arithmetic  3.64 us (2%)
    all_gather x1, waiting for transfers between devices, shards(): kt_all = lax.all_gather(kt, 'seq', axis=0, tiled=True)  49.8 us
    pallas_call x1, Pallas kernels, shards(): pl.pallas_call(functools.partial(attention_kernel, blocks=blocks, listed=...  47.9 us
    all_gather x1, waiting for transfers between devices, shards(): v_all = lax.all_gather(v, 'seq', axis=0, tiled=True)  46.5 us
    all_to_all x1, blocking collectives, shards(): lax.all_to_all(attended, 'head', split_axis=0, concat_axis=1, tiled=True)  29.2 us
  transfers between devices with their start and end apart: 2, of which 2 were waited for; matrix products, arithmetic and copies ran while one was open for 4% of the time, Pallas kernels for 0%

profile of v1, /device:TPU:0, one launch (start us, length us, event | category | flops | bytes accessed | tf_op | source)
XLA Modules:
  0.0 196.5 jit_solution(5595747487890436208)
XLA Ops:
  6.5 0.0 all-gather.5.cloned.1.call-start
  6.5 0.7 all-gather.5.cloned.1.call-update
  7.3 0.0 all-gather.3.cloned.1.call-start
  7.3 1.8 copy.11
  9.1 0.0 all-gather.3.cloned.1.call-update
  9.1 0.8 broadcast_subtract_fusion
  9.9 1.9 compare_reduce_fusion
  11.8 0.8 broadcast_compare_fusion
  12.6 0.1 broadcast_select_fusion
  12.7 0.7 select_n.19.bias_ref
  13.4 0.7 broadcast_in_dim.16
  14.0 0.1 add_select_fusion
  14.1 0.7 select_n.17.index_ref
  14.8 46.5 %all-gather.5.cloned.1.call-done.v_ref = bf16[64,128,128]{2,1,0:T(8,128)(2,1)} async-done(((bf16[8,128,128]{2,1,0:T(8,128)(2,1)}), bf16[64,128,128]{2,1,0:T(8,128)(2,1)}) %all-gather.5.cloned.1.call-update) | async-done | bytes 2097168 | tf_op jit(solution)/shard_map/all_gather | solution.py:85
  61.3 49.8 %all-gather.3.cloned.1.call-done.kt_ref = bf16[64,128,128]{2,1,0:T(8,128)(2,1)} async-done(((bf16[8,128,128]{2,1,0:T(8,128)(2,1)}), bf16[64,128,128]{2,1,0:T(8,128)(2,1)}) %all-gather.3.cloned.1.call-update) | async-done | bytes 2097168 | tf_op jit(solution)/shard_map/all_gather | solution.py:84
  111.1 47.9 %shard_map.55 = bf16[1024,1024]{1,0:T(8,128)(2,1)} custom-call(s32[1]{0:T(128)} %bitcast.slab_ref, s32[1024]{0:T(1024)} %select_n.17.index_ref, f32[1024]{0:T(1024)} %select_n.19.bias_ref, bf16[1024,1024]{1,0:T(8,128)(2,1)} %q_ref.1, bf16[64,128,128]{2,1,0:T(8,128)(2,1)} %all-gather.3.cloned.1.call-done.kt_ref, ...), custom_call_target="tpu_custom_call" | custom-call | tf_op jit(solution)/shard_map/pallas_call | solution.py:86
  159.0 29.2 %all_to_all.19 = bf16[4,256,1024]{2,1,0:T(8,128)(2,1)S(1)} all-to-all(bf16[4,256,1024]{2,1,0:T(8,128)(2,1)} %bitcast.9), channel_id=1, replica_groups=mesh['head'=4,'seq'=8] {'head'}, dimensions={0} | all-to-all | bytes 4194304 | tf_op jit(solution)/shard_map/all_to_all | solution.py:103
  188.2 1.5 copy.13
  (1 shorter events, 0.0 us)
Async XLA Ops:
  6.5 54.8 %all-gather.5.cloned.1.call-start = ((), (), s32[]{:S(2)}) async-start(), calls=%async_computation.2 | async-start | bytes 2359296 | tf_op jit(solution)/shard_map/all_gather | solution.py:85
  7.3 103.8 %all-gather.3.cloned.1.call-start = ((), (), s32[]{:S(2)}) async-start(), calls=%async_computation.1 | async-start | bytes 2359296 | tf_op jit(solution)/shard_map/all_gather | solution.py:84
Sparse Core Ops, SparseCore 0:
  9.5 51.7 all-gather.4
  63.4 47.6 all-gather.2

commit v2 on v1

v2 whole, which is shorter than its diff:
```python
import functools
import math

import jax
import jax.numpy as jnp
from jax import lax
from jax.experimental import pallas as pl
from jax.experimental.pallas import tpu as pltpu
from jax.sharding import PartitionSpec as P

BLK = 128
NEG = -1e30
PIECES = 2
MESH = pl.DeviceIdType.MESH


def attend_block(q, own, row, index_ref, bias_ref, kt_ref, v_ref, causal, listed, factor):
    scores = [jnp.where(causal, jnp.dot(q, kt_ref[own], preferred_element_type=jnp.float32), NEG)]
    for n in range(0, listed, 2):
        a, b = index_ref[row + n], index_ref[row + n + 1]
        pair = jnp.dot(
            q, jnp.concatenate([kt_ref[a], kt_ref[b]], axis=1), preferred_element_type=jnp.float32
        )
        scores.append(pair[:, :BLK] + bias_ref[row + n])
        scores.append(pair[:, BLK:] + bias_ref[row + n + 1])
    top = functools.reduce(jnp.maximum, scores)
    top = jnp.max(top, axis=1, keepdims=True) * factor
    total = None
    rounded = []
    for s in scores:
        w = jnp.exp2(s * factor - top)
        total = w if total is None else total + w
        rounded.append(w.astype(jnp.bfloat16))
    mixed = jnp.dot(rounded[0], v_ref[own], preferred_element_type=jnp.float32)
    for n in range(0, listed, 2):
        a, b = index_ref[row + n], index_ref[row + n + 1]
        mixed += jnp.dot(
            jnp.concatenate([rounded[1 + n], rounded[2 + n]], axis=1),
            jnp.concatenate([v_ref[a], v_ref[b]], axis=0),
            preferred_element_type=jnp.float32,
        )
    total = jnp.sum(total, axis=1, keepdims=True)
    return (mixed / total).astype(jnp.bfloat16)


def layer_kernel(
    index_ref,
    bias_ref,
    q_ref,
    kt_ref,
    v_ref,
    out_ref,
    kt_buf,
    v_buf,
    staged,
    load_sem,
    chain_send,
    chain_recv,
    cross_send,
    cross_recv,
    out_local,
    out_send,
    out_recv,
    *,
    blocks,
    listed,
    width,
    heads,
    slabs,
    groups,
):
    slab = lax.axis_index("seq")
    group = lax.axis_index("head")
    chain_len = slabs // 2
    place, side = slab // 2, slab % 2
    piece = blocks // PIECES
    bufs = (kt_buf, v_buf)
    has_next = place + 1 < chain_len

    def part(kv, place_of, side_of, c):
        first = pl.multiple_of((place_of * 2 + side_of) * blocks + c * piece, piece)
        return bufs[kv].at[pl.ds(first, piece)]

    def chain(t, kv, c):
        ref = part(kv, place - t, side, c)
        return pltpu.make_async_remote_copy(
            ref, ref, chain_send.at[t, kv, c], chain_recv.at[t, kv, c],
            device_id={"seq": slab + 2}, device_id_type=MESH,
        )

    def chain_in(t, kv, c):
        ref = part(kv, place - t, side, c)
        return pltpu.make_async_remote_copy(
            ref, ref, chain_send.at[t - 1, kv, c], chain_recv.at[t - 1, kv, c],
            device_id={"seq": slab - 2}, device_id_type=MESH,
        )

    def cross(t, kv, c, side_of):
        ref = part(kv, place - t, side_of, c)
        return pltpu.make_async_remote_copy(
            ref, ref, cross_send.at[t, kv, c], cross_recv.at[t, kv, c],
            device_id={"seq": place * 2 + 1 - side}, device_id_type=MESH,
        )

    def sends_cross(t):
        return side == 0 if t == 0 else place >= t

    def gets_cross(t):
        return side == 1 if t == 0 else place >= t

    own_first = pl.multiple_of(slab * blocks, blocks)
    loads = [
        pltpu.make_async_copy(src, buf.at[pl.ds(own_first, blocks)], load_sem.at[kv])
        for kv, (src, buf) in enumerate(((kt_ref, kt_buf), (v_ref, v_buf)))
    ]
    for load in loads:
        load.start()

    barrier = pltpu.get_barrier_semaphore()
    pl.semaphore_signal(
        barrier, 1, device_id={"seq": place * 2 + 1 - side}, device_id_type=MESH
    )
    for d in range(1, groups):
        pl.semaphore_signal(
            barrier, 1, device_id={"head": lax.rem(group + d, groups)}, device_id_type=MESH
        )

    @pl.when(has_next)
    def _():
        pl.semaphore_signal(barrier, 1, device_id={"seq": slab + 2}, device_id_type=MESH)

    @pl.when(place > 0)
    def _():
        pl.semaphore_signal(barrier, 1, device_id={"seq": slab - 2}, device_id_type=MESH)

    pl.semaphore_wait(
        barrier, groups + has_next.astype(jnp.int32) + (place > 0).astype(jnp.int32)
    )
    for load in loads:
        load.wait()

    for kv in range(2):
        for t in range(chain_len):
            for c in range(PIECES):
                if t > 0:

                    @pl.when(place >= t)
                    def _():
                        chain_in(t, kv, c).wait_recv()

                if t < chain_len - 1:

                    @pl.when((place >= t) & has_next)
                    def _():
                        chain(t, kv, c).start()

                @pl.when(sends_cross(t))
                def _():
                    cross(t, kv, c, side).start()

    for kv in range(2):
        for t in range(chain_len):
            for c in range(PIECES):

                @pl.when(gets_cross(t))
                def _():
                    cross(t, kv, c, 1 - side).wait_recv()

    factor = math.log2(math.e) / math.sqrt(width)
    causal = lax.broadcasted_iota(jnp.int32, (BLK, BLK), 0) >= lax.broadcasted_iota(
        jnp.int32, (BLK, BLK), 1
    )
    share = blocks // groups
    share_rows = share * BLK
    base = slab * blocks

    def out_columns(group_of, head):
        return pl.ds(pl.multiple_of((group_of * heads + head) * width, width), width)

    def out_copy(head, r):
        owner = lax.rem(group + 1 + r, groups)
        return pltpu.make_async_remote_copy(
            staged.at[head, pl.ds(pl.multiple_of(owner * share_rows, share_rows), share_rows)],
            out_ref.at[:, out_columns(group, head)],
            out_send.at[head, r], out_recv.at[head, r],
            device_id={"head": owner}, device_id_type=MESH,
        )

    def out_in(head, r):
        sender = lax.rem(group + groups - 1 - r, groups)
        return pltpu.make_async_remote_copy(
            staged.at[head, pl.ds(0, share_rows)],
            out_ref.at[:, out_columns(sender, head)],
            out_send.at[head, r], out_recv.at[head, r],
            device_id={"head": sender}, device_id_type=MESH,
        )

    def out_own(head):
        return pltpu.make_async_copy(
            staged.at[head, pl.ds(pl.multiple_of(group * share_rows, share_rows), share_rows)],
            out_ref.at[:, out_columns(group, head)],
            out_local.at[head],
        )

    def one_share(step, carry):
        head, r = step // groups, step % groups
        owner = lax.rem(group + 1 + r, groups)
        columns = pl.ds(pl.multiple_of(head * width, width), width)
        for u in range(share):
            i = owner * share + u
            rows = pl.ds(pl.multiple_of(i * BLK, BLK), BLK)
            row = (head * blocks + i) * listed
            staged[head, rows, :] = attend_block(
                q_ref[rows, columns], base + i, row, index_ref, bias_ref, kt_buf, v_buf,
                causal, listed, factor,
            )

        @pl.when(r < groups - 1)
        def _():
            out_copy(head, r).start()

        @pl.when(r == groups - 1)
        def _():
            out_own(head).start()

        return carry

    lax.fori_loop(0, heads * groups, one_share, 0)

    for kv in range(2):
        for t in range(chain_len):
            for c in range(PIECES):
                if t < chain_len - 1:

                    @pl.when((place >= t) & has_next)
                    def _():
                        chain(t, kv, c).wait_send()

                @pl.when(sends_cross(t))
                def _():
                    cross(t, kv, c, side).wait_send()

    def finish(head, carry):
        out_own(head).wait()
        for r in range(groups - 1):
            out_copy(head, r).wait_send()
            out_in(head, r).wait_recv()
        return carry

    lax.fori_loop(0, heads, finish, 0)


def block_lists(vertical, slash, slab_index, blocks):
    ids = slab_index * blocks + jnp.arange(blocks, dtype=jnp.int32)
    slash_ids = ids[None, :, None] - slash[:, None, :]
    slash_ok = slash_ids >= 0
    columns = jnp.broadcast_to(vertical[:, None, :], slash_ids.shape[:2] + vertical.shape[1:])
    covered = jnp.any(columns[..., None] == slash_ids[:, :, None, :], axis=3)
    column_ok = (columns < ids[None, :, None]) & jnp.logical_not(covered)
    listed = jnp.concatenate([slash_ids, columns], axis=2)
    ok = jnp.concatenate([slash_ok, column_ok], axis=2)
    index = jnp.where(ok, listed, ids[None, :, None])
    bias = jnp.where(ok, 0.0, NEG).astype(jnp.float32)
    return index.reshape(-1), bias.reshape(-1), listed.shape[2]


def shards(queries, keys, values, vertical, slash):
    width = keys.shape[1]
    rows = queries.shape[0]
    blocks = rows // BLK
    heads = vertical.shape[0]
    slabs, groups = lax.axis_size("seq"), lax.axis_size("head")
    kt = jnp.swapaxes(keys.reshape(blocks, BLK, width), 1, 2)
    v = values.reshape(blocks, BLK, width)
    index, bias, listed = block_lists(vertical, slash, lax.axis_index("seq"), blocks)
    dma = pltpu.SemaphoreType.DMA
    hops = (slabs // 2, 2, PIECES)
    smem, anywhere = pl.BlockSpec(memory_space=pltpu.SMEM), pl.BlockSpec(memory_space=pl.ANY)
    return pl.pallas_call(
        functools.partial(
            layer_kernel,
            blocks=blocks,
            listed=listed,
            width=width,
            heads=heads,
            slabs=slabs,
            groups=groups,
        ),
        in_specs=[smem, smem, pl.BlockSpec(memory_space=pltpu.VMEM), anywhere, anywhere],
        out_specs=anywhere,
        out_shape=jax.ShapeDtypeStruct((rows // groups, groups * heads * width), jnp.bfloat16),
        scratch_shapes=[
            pltpu.VMEM((slabs * blocks, width, BLK), jnp.bfloat16),
            pltpu.VMEM((slabs * blocks, BLK, width), jnp.bfloat16),
            pltpu.VMEM((heads, rows, width), jnp.bfloat16),
            dma((2,)),
            dma(hops),
            dma(hops),
            dma(hops),
            dma(hops),
            dma((heads,)),
            dma((heads, groups - 1)),
            dma((heads, groups - 1)),
        ],
        compiler_params=pltpu.CompilerParams(
            collective_id=0, has_side_effects=True, vmem_limit_bytes=60 * 1024 * 1024
        ),
    )(index, bias, queries, kt, v)


def solution(mesh):
    in_specs = (
        P("seq", "head"),
        P("seq", "head"),
        P("seq", "head"),
        P("head", None),
        P("head", None),
    )
    out_specs = P(("seq", "head"), None)
    return jax.shard_map(shards, mesh=mesh, in_specs=in_specs, out_specs=out_specs, check_vma=False)
```

time: 197 us -> 108 us (0.55)
  the two profiles are of different devices: /device:TPU:0 before, /device:TPU:27 now
where the time goes in v2:
time: 108 us
  Pallas kernels  96.9 us (90%)
  local copies, waits for them, and re-layouts  6.96 us (6%)
  other arithmetic  3.63 us (3%)
    pallas_call x1, Pallas kernels, shards(): pl.pallas_call(functools.partial(layer_kernel, blocks=blocks, listed=list...  96.9 us
    unnamed x1, local copies, waits for them, and re-layouts  3.13 us

profile of v2, /device:TPU:27, one launch (start us, length us, event | category | flops | bytes accessed | tf_op | source)
XLA Modules:
  0.0 107.5 jit_solution(16154341253551571111)
XLA Ops:
  0.0 0.8 broadcast_subtract_fusion
  0.8 1.9 %compare_reduce_fusion = pred[8,8,8]{2,1,0:T(8,128)(4,1)S(1)} fusion(s32[8,8,8]{2,1,0:T(8,128)S(1)} %broadcast_subtract_fusion, s32[8,8]{1,0:T(8,128)} %param.8), kind=kLoop, calls=%fused_computation | loop fusion | flops 7680 | bytes 2816 | tf_op jit(solution)/shard_map/reduce_or | solution.py:258
  2.7 0.8 broadcast_compare_fusion
  3.5 0.1 broadcast_select_fusion
  3.6 0.7 select_n.19.bias_ref
  4.2 0.7 broadcast_in_dim.16
  4.9 0.1 add_select_fusion
  5.0 0.7 select_n.17.index_ref
  5.7 1.8 %copy.7 = bf16[8,128,128]{1,2,0:T(8,128)(2,1)} copy(bf16[8,128,128]{2,1,0:T(8,128)(2,1)} %bitcast.5) | data formatting | bytes 524288 | tf_op jit(solution)/shard_map/reshape | solution.py:273
  7.5 96.9 %shard_map.55 = bf16[256,4096]{1,0:T(8,128)(2,1)} custom-call(s32[1024]{0:T(1024)} %select_n.17.index_ref, f32[1024]{0:T(1024)} %select_n.19.bias_ref, bf16[1024,1024]{1,0:T(8,128)(2,1)} %q_ref.1, bf16[8,128,128]{2,1,0:T(8,128)(2,1)} %bitcast.3, bf16[8,128,128]{2,1,0:T(8,128)(2,1)} %bitcast.4), custom_call_target="tpu_custom_call" | custom-call | tf_op jit(solution)/shard_map/pallas_call | solution.py:279
  104.4 3.1 %copy.9 = bf16[256,4096]{1,0:T(8,128)(2,1)} copy(bf16[256,4096]{1,0:T(8,128)(2,1)} %shard_map.55) | data formatting | bytes 4194304
  (1 shorter events, 0.0 us)

commit v3 on v2

--- a/solution.py
+++ b/solution.py
@@ -11,10 +11,12 @@
 BLK = 128
 NEG = -1e30
 PIECES = 2
+EARLY = 6
+VALUE_STRIDE = 3
 MESH = pl.DeviceIdType.MESH
 
 
-def attend_block(q, own, row, index_ref, bias_ref, kt_ref, v_ref, causal, listed, factor):
+def block_weights(q, own, row, index_ref, bias_ref, kt_ref, causal, listed, factor):
     scores = [jnp.where(causal, jnp.dot(q, kt_ref[own], preferred_element_type=jnp.float32), NEG)]
     for n in range(0, listed, 2):
         a, b = index_ref[row + n], index_ref[row + n + 1]
@@ -31,28 +33,36 @@
         w = jnp.exp2(s * factor - top)
         total = w if total is None else total + w
         rounded.append(w.astype(jnp.bfloat16))
-    mixed = jnp.dot(rounded[0], v_ref[own], preferred_element_type=jnp.float32)
+    return rounded, jnp.sum(total, axis=1, keepdims=True)
+
+
+def block_mix(own_weights, pair_weights, total, own, row, index_ref, v_ref, listed):
+    mixed = jnp.dot(own_weights, v_ref[own], preferred_element_type=jnp.float32)
     for n in range(0, listed, 2):
         a, b = index_ref[row + n], index_ref[row + n + 1]
         mixed += jnp.dot(
-            jnp.concatenate([rounded[1 + n], rounded[2 + n]], axis=1),
+            pair_weights(n),
             jnp.concatenate([v_ref[a], v_ref[b]], axis=0),
             preferred_element_type=jnp.float32,
         )
-    total = jnp.sum(total, axis=1, keepdims=True)
     return (mixed / total).astype(jnp.bfloat16)
 
 
 def layer_kernel(
+    slash_ref,
+    vertical_ref,
+    queries_ref,
+    kt_ref,
+    v_ref,
+    out_ref,
     index_ref,
     bias_ref,
     q_ref,
-    kt_ref,
-    v_ref,
-    out_ref,
     kt_buf,
     v_buf,
     staged,
+    early_weights,
+    early_total,
     load_sem,
     chain_send,
     chain_recv,
@@ -113,6 +123,7 @@
         pltpu.make_async_copy(src, buf.at[pl.ds(own_first, blocks)], load_sem.at[kv])
         for kv, (src, buf) in enumerate(((kt_ref, kt_buf), (v_ref, v_buf)))
     ]
+    loads.append(pltpu.make_async_copy(queries_ref, q_ref, load_sem.at[2]))
     for load in loads:
         load.start()
 
@@ -136,35 +147,62 @@
     pl.semaphore_wait(
         barrier, groups + has_next.astype(jnp.int32) + (place > 0).astype(jnp.int32)
     )
-    for load in loads:
-        load.wait()
-
-    for kv in range(2):
-        for t in range(chain_len):
-            for c in range(PIECES):
-                if t > 0:
-
-                    @pl.when(place >= t)
-                    def _():
-                        chain_in(t, kv, c).wait_recv()
-
-                if t < chain_len - 1:
-
-                    @pl.when((place >= t) & has_next)
-                    def _():
-                        chain(t, kv, c).start()
-
-                @pl.when(sends_cross(t))
-                def _():
-                    cross(t, kv, c, side).start()
-
-    for kv in range(2):
+    def pass_on(t, kv, c):
+        if t > 0:
+
+            @pl.when(place >= t)
+            def _():
+                chain_in(t, kv, c).wait_recv()
+
+        if t < chain_len - 1:
+
+            @pl.when((place >= t) & has_next)
+            def _():
+                chain(t, kv, c).start()
+
+        @pl.when(sends_cross(t))
+        def _():
+            cross(t, kv, c, side).start()
+
+    def wait_cross(kv):
         for t in range(chain_len):
             for c in range(PIECES):
 
                 @pl.when(gets_cross(t))
                 def _():
                     cross(t, kv, c, 1 - side).wait_recv()
+
+    base = slab * blocks
+    slashes, verticals = slash_ref.shape[1], vertical_ref.shape[1]
+
+    def list_blocks(step, carry):
+        head, own = step // blocks, base + step % blocks
+        reached = [own - slash_ref[head, n] for n in range(slashes)]
+        for n, block in enumerate(reached):
+            ok = block >= 0
+            index_ref[step * listed + n] = jnp.where(ok, block, own)
+            bias_ref[step * listed + n] = jnp.where(ok, 0.0, NEG)
+        for n in range(verticals):
+            block = vertical_ref[head, n]
+            ok = block < own
+            for other in reached:
+                ok = ok & (block != other)
+            index_ref[step * listed + slashes + n] = jnp.where(ok, block, own)
+            bias_ref[step * listed + slashes + n] = jnp.where(ok, 0.0, NEG)
+        return carry
+
+    loads[0].wait()
+    for c in range(PIECES):
+        pass_on(0, 0, c)
+    lax.fori_loop(0, heads * blocks, list_blocks, 0)
+    for t in range(1, chain_len):
+        for c in range(PIECES):
+            pass_on(t, 0, c)
+    loads[1].wait()
+    for c in range(PIECES):
+        pass_on(0, 1, c)
+    wait_cross(0)
+    loads[2].wait()
 
     factor = math.log2(math.e) / math.sqrt(width)
     causal = lax.broadcasted_iota(jnp.int32, (BLK, BLK), 0) >= lax.broadcasted_iota(
@@ -172,7 +210,6 @@
     )
     share = blocks // groups
     share_rows = share * BLK
-    base = slab * blocks
 
     def out_columns(group_of, head):
         return pl.ds(pl.multiple_of((group_of * heads + head) * width, width), width)
@@ -202,18 +239,20 @@
             out_local.at[head],
         )
 
-    def one_share(step, carry):
+    early = early_weights.shape[0]
+    values_due = [(t, c) for t in range(1, chain_len) for c in range(PIECES)]
+
+    def owned_blocks(step):
         head, r = step // groups, step % groups
         owner = lax.rem(group + 1 + r, groups)
         columns = pl.ds(pl.multiple_of(head * width, width), width)
         for u in range(share):
             i = owner * share + u
             rows = pl.ds(pl.multiple_of(i * BLK, BLK), BLK)
-            row = (head * blocks + i) * listed
-            staged[head, rows, :] = attend_block(
-                q_ref[rows, columns], base + i, row, index_ref, bias_ref, kt_buf, v_buf,
-                causal, listed, factor,
-            )
+            yield head, rows, columns, base + i, (head * blocks + i) * listed
+
+    def send_share(step):
+        head, r = step // groups, step % groups
 
         @pl.when(r < groups - 1)
         def _():
@@ -223,9 +262,51 @@
         def _():
             out_own(head).start()
 
-        return carry
-
-    lax.fori_loop(0, heads * groups, one_share, 0)
+    def weigh_early(step, carry):
+        for k, (t, c) in enumerate(values_due):
+
+            @pl.when(step == min(VALUE_STRIDE * (k + 1), early * groups - 1))
+            def _():
+                pass_on(t, 1, c)
+
+        for head, rows, columns, own, row in owned_blocks(step):
+            rounded, total = block_weights(
+                q_ref[rows, columns], own, row, index_ref, bias_ref, kt_buf, causal, listed, factor
+            )
+            for n, w in enumerate(rounded):
+                early_weights[head, rows, n * BLK : (n + 1) * BLK] = w
+            early_total[head, rows, :] = jnp.broadcast_to(total, (BLK, width))
+        return carry
+
+    def mix_early(step, carry):
+        for head, rows, columns, own, row in owned_blocks(step):
+            staged[head, rows, :] = block_mix(
+                early_weights[head, rows, :BLK],
+                lambda n: early_weights[head, rows, (n + 1) * BLK : (n + 3) * BLK],
+                early_total[head, rows, :],
+                own, row, index_ref, v_buf, listed,
+            )
+        send_share(step)
+        return carry
+
+    def one_share(step, carry):
+        for head, rows, columns, own, row in owned_blocks(step):
+            rounded, total = block_weights(
+                q_ref[rows, columns], own, row, index_ref, bias_ref, kt_buf, causal, listed, factor
+            )
+            staged[head, rows, :] = block_mix(
+                rounded[0],
+                lambda n: jnp.concatenate([rounded[1 + n], rounded[2 + n]], axis=1),
+                total,
+                own, row, index_ref, v_buf, listed,
+            )
+        send_share(step)
+        return carry
+
+    lax.fori_loop(0, early * groups, weigh_early, 0)
+    wait_cross(1)
+    lax.fori_loop(0, early * groups, mix_early, 0)
+    lax.fori_loop(early * groups, heads * groups, one_share, 0)
 
     for kv in range(2):
         for t in range(chain_len):
@@ -248,20 +329,6 @@
         return carry
 
     lax.fori_loop(0, heads, finish, 0)
-
-
-def block_lists(vertical, slash, slab_index, blocks):
-    ids = slab_index * blocks + jnp.arange(blocks, dtype=jnp.int32)
-    slash_ids = ids[None, :, None] - slash[:, None, :]
-    slash_ok = slash_ids >= 0
-    columns = jnp.broadcast_to(vertical[:, None, :], slash_ids.shape[:2] + vertical.shape[1:])
-    covered = jnp.any(columns[..., None] == slash_ids[:, :, None, :], axis=3)
-    column_ok = (columns < ids[None, :, None]) & jnp.logical_not(covered)
-    listed = jnp.concatenate([slash_ids, columns], axis=2)
-    ok = jnp.concatenate([slash_ok, column_ok], axis=2)
-    index = jnp.where(ok, listed, ids[None, :, None])
-    bias = jnp.where(ok, 0.0, NEG).astype(jnp.float32)
-    return index.reshape(-1), bias.reshape(-1), listed.shape[2]
 
 
 def shards(queries, keys, values, vertical, slash):
@@ -272,7 +339,8 @@
     slabs, groups = lax.axis_size("seq"), lax.axis_size("head")
     kt = jnp.swapaxes(keys.reshape(blocks, BLK, width), 1, 2)
     v = values.reshape(blocks, BLK, width)
-    index, bias, listed = block_lists(vertical, slash, lax.axis_index("seq"), blocks)
+    listed = slash.shape[1] + vertical.shape[1]
+    early = min(EARLY, heads)
     dma = pltpu.SemaphoreType.DMA
     hops = (slabs // 2, 2, PIECES)
     smem, anywhere = pl.BlockSpec(memory_space=pltpu.SMEM), pl.BlockSpec(memory_space=pl.ANY)
@@ -286,14 +354,19 @@
             slabs=slabs,
             groups=groups,
         ),
-        in_specs=[smem, smem, pl.BlockSpec(memory_space=pltpu.VMEM), anywhere, anywhere],
+        in_specs=[smem, smem, anywhere, anywhere, anywhere],
         out_specs=anywhere,
         out_shape=jax.ShapeDtypeStruct((rows // groups, groups * heads * width), jnp.bfloat16),
         scratch_shapes=[
+            pltpu.SMEM((heads * blocks * listed,), jnp.int32),
+            pltpu.SMEM((heads * blocks * listed,), jnp.float32),
+            pltpu.VMEM(queries.shape, jnp.bfloat16),
             pltpu.VMEM((slabs * blocks, width, BLK), jnp.bfloat16),
             pltpu.VMEM((slabs * blocks, BLK, width), jnp.bfloat16),
             pltpu.VMEM((heads, rows, width), jnp.bfloat16),
-            dma((2,)),
+            pltpu.VMEM((early, rows, (listed + 1) * BLK), jnp.bfloat16),
+            pltpu.VMEM((early, rows, width), jnp.float32),
+            dma((3,)),
             dma(hops),
             dma(hops),
             dma(hops),
@@ -303,9 +376,9 @@
             dma((heads, groups - 1)),
         ],
         compiler_params=pltpu.CompilerParams(
-            collective_id=0, has_side_effects=True, vmem_limit_bytes=60 * 1024 * 1024
+            collective_id=0, has_side_effects=True, vmem_limit_bytes=62 * 1024 * 1024
         ),
-    )(index, bias, queries, kt, v)
+    )(slash, vertical, queries, kt, v)
 
 
 def solution(mesh):

time: 108 us -> 80.3 us (0.74)
  Pallas kernels: 96.9 us -> 75 us
  other arithmetic: 3.63 us -> 0 us
  local copies, waits for them, and re-layouts: 6.96 us -> 4.92 us
    pallas_call x1, Pallas kernels: 96.9 us -> 75 us  [shards(): pl.pallas_call(functools.partial(layer_kernel, blocks=blocks, listed=list...]
    reduce_or x1 -> x0, other arithmetic: 1.91 us -> none  [block_lists(): covered = jnp.any(columns[..., None] == slash_ids[:, :, None, :], axis=3)]
    select_n x2 -> x0, local copies, waits for them, and re-layouts: 1.35 us -> none  [the longest x1 0.68 us: block_lists(): index = jnp.where(ok, listed, ids[None, :, None])]
where the time goes in v3:
time: 80.3 us; the launch traced here: 79.9 us
  Pallas kernels  75 us (93%)
  local copies, waits for them, and re-layouts  4.92 us (6%)
    pallas_call x1, Pallas kernels, shards(): pl.pallas_call(functools.partial(layer_kernel, blocks=blocks, listed=list...  75 us
    unnamed x1, local copies, waits for them, and re-layouts  3.13 us
    reshape x1, local copies, waits for them, and re-layouts, shards(): kt = jnp.swapaxes(keys.reshape(blocks, BLK, width), 1, 2)  1.79 us

profile of v3, /device:TPU:27, one launch (start us, length us, event | category | flops | bytes accessed | tf_op | source)
XLA Modules:
  0.0 79.9 jit_solution(436473033521152419)
XLA Ops:
  0.0 1.8 %copy.6 = bf16[8,128,128]{1,2,0:T(8,128)(2,1)} copy(bf16[8,128,128]{2,1,0:T(8,128)(2,1)} %bitcast.5) | data formatting | bytes 524288 | tf_op jit(solution)/shard_map/reshape | solution.py:340
  1.8 75.0 %shard_map.55 = bf16[256,4096]{1,0:T(8,128)(2,1)} custom-call(s32[8,8]{1,0:T(8,128)} %slash_ref.1, s32[8,8]{1,0:T(8,128)} %vertical_ref.1, bf16[1024,1024]{1,0:T(8,128)(2,1)} %queries_ref.1, bf16[8,128,128]{2,1,0:T(8,128)(2,1)} %bitcast.3, bf16[8,128,128]{2,1,0:T(8,128)(2,1)} %bitcast.4), custom_call_target="tpu_custom_call" | custom-call | tf_op jit(solution)/shard_map/pallas_call | solution.py:347
  76.8 3.1 %copy.8 = bf16[256,4096]{1,0:T(8,128)(2,1)} copy(bf16[256,4096]{1,0:T(8,128)(2,1)} %shard_map.55) | data formatting | bytes 4194304

commit v4 on v3

--- a/solution.py
+++ b/solution.py
@@ -9,6 +9,8 @@
 from jax.sharding import PartitionSpec as P
 
 BLK = 128
+LARGEST_OFFSET = 28
+CAP = 4
 NEG = -1e30
 PIECES = 2
 EARLY = 6
@@ -57,12 +59,19 @@
     out_ref,
     index_ref,
     bias_ref,
+    rank_ref,
+    used_ref,
+    found_ref,
+    pack_ref,
     q_ref,
     kt_buf,
     v_buf,
     staged,
     early_weights,
     early_total,
+    held,
+    packed,
+    held_sem,
     load_sem,
     chain_send,
     chain_recv,
@@ -87,36 +96,55 @@
     bufs = (kt_buf, v_buf)
     has_next = place + 1 < chain_len
 
-    def part(kv, place_of, side_of, c):
-        first = pl.multiple_of((place_of * 2 + side_of) * blocks + c * piece, piece)
+    whole_blocks = slabs * blocks
+    reach = (LARGEST_OFFSET + blocks - 1) // blocks
+    pack_at = reach // 2
+    cap_piece = CAP // PIECES
+
+    def part(kv, place_of, side_of, c, far):
+        origin = place_of * 2 + side_of
+        if far:
+            first = pl.multiple_of(whole_blocks + origin * CAP + c * cap_piece, cap_piece)
+            return bufs[kv].at[pl.ds(first, cap_piece)]
+        first = pl.multiple_of(origin * blocks + c * piece, piece)
         return bufs[kv].at[pl.ds(first, piece)]
 
+    def sent(ref, t, kv, c, far):
+        if t == pack_at and far:
+            return packed.at[kv, pl.ds(c * cap_piece, cap_piece)]
+        return ref
+
     def chain(t, kv, c):
-        ref = part(kv, place - t, side, c)
+        ref = part(kv, place - t, side, c, chain_far(t + 1))
         return pltpu.make_async_remote_copy(
-            ref, ref, chain_send.at[t, kv, c], chain_recv.at[t, kv, c],
+            sent(ref, t, kv, c, chain_far(t + 1)), ref, chain_send.at[t, kv, c], chain_recv.at[t, kv, c],
             device_id={"seq": slab + 2}, device_id_type=MESH,
         )
 
     def chain_in(t, kv, c):
-        ref = part(kv, place - t, side, c)
+        ref = part(kv, place - t, side, c, chain_far(t))
         return pltpu.make_async_remote_copy(
             ref, ref, chain_send.at[t - 1, kv, c], chain_recv.at[t - 1, kv, c],
             device_id={"seq": slab - 2}, device_id_type=MESH,
         )
 
-    def cross(t, kv, c, side_of):
-        ref = part(kv, place - t, side_of, c)
+    def cross(t, kv, c, sender):
+        ref = part(kv, place - t, sender, c, cross_far(t, sender))
         return pltpu.make_async_remote_copy(
-            ref, ref, cross_send.at[t, kv, c], cross_recv.at[t, kv, c],
+            sent(ref, t, kv, c, cross_far(t, sender)), ref, cross_send.at[t, kv, c], cross_recv.at[t, kv, c],
             device_id={"seq": place * 2 + 1 - side}, device_id_type=MESH,
         )
 
-    def sends_cross(t):
-        return side == 0 if t == 0 else place >= t
-
-    def gets_cross(t):
-        return side == 1 if t == 0 else place >= t
+    def chain_far(t):
+        return 2 * t > reach
+
+    def cross_far(t, sender):
+        return (2 * t - 1 if sender else 2 * t + 1) > reach
+
+    def cross_runs(t, sender, this_side):
+        if t == 0 and sender == 1:
+            return None
+        return (side == this_side) & (place >= t)
 
     own_first = pl.multiple_of(slab * blocks, blocks)
     loads = [
@@ -147,6 +175,22 @@
     pl.semaphore_wait(
         barrier, groups + has_next.astype(jnp.int32) + (place > 0).astype(jnp.int32)
     )
+    def start_cross(t, kv, c, packed):
+        for sender in range(2):
+            runs = cross_runs(t, sender, sender)
+            if runs is not None and (t == pack_at and cross_far(t, sender)) == packed:
+
+                @pl.when(runs)
+                def _():
+                    cross(t, kv, c, sender).start()
+
+    def start_chain(t, kv, c, packed):
+        if t < chain_len - 1 and (t == pack_at and chain_far(t + 1)) == packed:
+
+            @pl.when((place >= t) & has_next)
+            def _():
+                chain(t, kv, c).start()
+
     def pass_on(t, kv, c):
         if t > 0:
 
@@ -154,26 +198,60 @@
             def _():
                 chain_in(t, kv, c).wait_recv()
 
-        if t < chain_len - 1:
-
-            @pl.when((place >= t) & has_next)
+        start_chain(t, kv, c, False)
+        start_cross(t, kv, c, False)
+        if t == pack_at and c == PIECES - 1:
+
+            @pl.when(place >= t)
             def _():
-                chain(t, kv, c).start()
-
-        @pl.when(sends_cross(t))
-        def _():
-            cross(t, kv, c, side).start()
+                first = pl.multiple_of(((place - t) * 2 + side) * blocks, blocks)
+                move = pltpu.make_async_copy(
+                    bufs[kv].at[pl.ds(first, blocks)], held.at[kv], held_sem.at[kv]
+                )
+                move.start()
+                move.wait()
+                for k in range(CAP):
+                    picked = held[kv, 0].astype(jnp.float32) * pack_ref[k * blocks]
+                    for n in range(1, blocks):
+                        picked += held[kv, n].astype(jnp.float32) * pack_ref[k * blocks + n]
+                    packed[kv, k] = picked.astype(jnp.bfloat16)
+
+            for each in range(PIECES):
+                start_chain(t, kv, each, True)
+                start_cross(t, kv, each, True)
 
     def wait_cross(kv):
         for t in range(chain_len):
             for c in range(PIECES):
-
-                @pl.when(gets_cross(t))
-                def _():
-                    cross(t, kv, c, 1 - side).wait_recv()
+                for sender in range(2):
+                    runs = cross_runs(t, sender, 1 - sender)
+                    if runs is not None:
+
+                        @pl.when(runs)
+                        def _():
+                            cross(t, kv, c, sender).wait_recv()
 
     base = slab * blocks
     slashes, verticals = slash_ref.shape[1], vertical_ref.shape[1]
+
+    def rank_block(block, rank):
+        used = block < 0
+        for head in range(heads):
+            for n in range(verticals):
+                used = used | (vertical_ref[head, n] == block)
+        rank = jnp.where(block % blocks == 0, 0, rank)
+        rank_ref[block] = rank
+        used_ref[block] = used.astype(jnp.int32)
+        return rank + used.astype(jnp.int32)
+
+    def place_verticals(head, carry):
+        for n in range(verticals):
+            block = vertical_ref[head, n]
+            far = whole_blocks + (block // blocks) * CAP + rank_ref[block]
+            found_ref[head * verticals + n] = jnp.where(
+                block >= (slab - reach) * blocks, block, far
+            )
+        return carry
 
     def list_blocks(step, carry):
         head, own = step // blocks, base + step % blocks
@@ -187,20 +265,34 @@
             ok = block < own
             for other in reached:
                 ok = ok & (block != other)
-            index_ref[step * listed + slashes + n] = jnp.where(ok, block, own)
+            found = found_ref[head * verticals + n]
+            index_ref[step * listed + slashes + n] = jnp.where(ok, found, own)
             bias_ref[step * listed + slashes + n] = jnp.where(ok, 0.0, NEG)
         return carry
 
+    lists = heads * blocks
     loads[0].wait()
     for c in range(PIECES):
         pass_on(0, 0, c)
-    lax.fori_loop(0, heads * blocks, list_blocks, 0)
+    lax.fori_loop(0, whole_blocks, rank_block, jnp.int32(0))
+    packed_first = jnp.maximum((place - pack_at) * 2 + side, 0) * blocks
+    for k in range(CAP):
+        for n in range(blocks):
+            block = packed_first + n
+            hit = (used_ref[block] == 1) & (rank_ref[block] == k)
+            pack_ref[k * blocks + n] = jnp.where(hit, 1.0, 0.0)
     for t in range(1, chain_len):
         for c in range(PIECES):
             pass_on(t, 0, c)
+        if t == 1:
+            lax.fori_loop(0, heads, place_verticals, 0)
+            lax.fori_loop(0, lists // 4, list_blocks, 0)
+        if t == 2:
+            lax.fori_loop(lists // 4, lists // 2, list_blocks, 0)
     loads[1].wait()
     for c in range(PIECES):
         pass_on(0, 1, c)
+    lax.fori_loop(lists // 2, lists, list_blocks, 0)
     wait_cross(0)
     loads[2].wait()
 
@@ -240,7 +332,10 @@
         )
 
     early = early_weights.shape[0]
-    values_due = [(t, c) for t in range(1, chain_len) for c in range(PIECES)]
+    values_due = []
+    for t in range(1, chain_len):
+        each = [[(t, c)] for c in range(PIECES)]
+        values_due += [sum(each, [])] if t == pack_at else each
 
     def owned_blocks(step):
         head, r = step // groups, step % groups
@@ -263,11 +358,12 @@
             out_own(head).start()
 
     def weigh_early(step, carry):
-        for k, (t, c) in enumerate(values_due):
+        for k, due in enumerate(values_due):
 
             @pl.when(step == min(VALUE_STRIDE * (k + 1), early * groups - 1))
             def _():
-                pass_on(t, 1, c)
+                for t, c in due:
+                    pass_on(t, 1, c)
 
         for head, rows, columns, own, row in owned_blocks(step):
             rounded, total = block_weights(
@@ -317,9 +413,13 @@
                     def _():
                         chain(t, kv, c).wait_send()
 
-                @pl.when(sends_cross(t))
-                def _():
-                    cross(t, kv, c, side).wait_send()
+                for sender in range(2):
+                    runs = cross_runs(t, sender, sender)
+                    if runs is not None:
+
+                        @pl.when(runs)
+                        def _():
+                            cross(t, kv, c, sender).wait_send()
 
     def finish(head, carry):
         out_own(head).wait()
@@ -360,12 +460,19 @@
         scratch_shapes=[
             pltpu.SMEM((heads * blocks * listed,), jnp.int32),
             pltpu.SMEM((heads * blocks * listed,), jnp.float32),
+            pltpu.SMEM((slabs * blocks,), jnp.int32),
+            pltpu.SMEM((slabs * blocks,), jnp.int32),
+            pltpu.SMEM((vertical.size,), jnp.int32),
+            pltpu.SMEM((CAP * blocks,), jnp.float32),
             pltpu.VMEM(queries.shape, jnp.bfloat16),
-            pltpu.VMEM((slabs * blocks, width, BLK), jnp.bfloat16),
-            pltpu.VMEM((slabs * blocks, BLK, width), jnp.bfloat16),
+            pltpu.VMEM((slabs * (blocks + CAP), width, BLK), jnp.bfloat16),
+            pltpu.VMEM((slabs * (blocks + CAP), BLK, width), jnp.bfloat16),
             pltpu.VMEM((heads, rows, width), jnp.bfloat16),
             pltpu.VMEM((early, rows, (listed + 1) * BLK), jnp.bfloat16),
             pltpu.VMEM((early, rows, width), jnp.float32),
+            pltpu.VMEM((2, blocks, BLK, width), jnp.bfloat16),
+            pltpu.VMEM((2, CAP, BLK, width), jnp.bfloat16),
+            dma((2,)),
             dma((3,)),
             dma(hops),
             dma(hops),

time: 80.3 us -> 78.2 us (0.974)
  Pallas kernels: 75 us -> 72.4 us
    pallas_call x1, Pallas kernels: 75 us -> 72.4 us  [shards(): pl.pallas_call(functools.partial(layer_kernel, blocks=blocks, listed=list...]
where the time goes in v4:
time: 78.2 us; the launch traced here: 77.4 us
  Pallas kernels  72.4 us (93%)
  local copies, waits for them, and re-layouts  4.92 us (6%)
    pallas_call x1, Pallas kernels, shards(): pl.pallas_call(functools.partial(layer_kernel, blocks=blocks, listed=list...  72.4 us
    unnamed x1, local copies, waits for them, and re-layouts  3.13 us
    reshape x1, local copies, waits for them, and re-layouts, shards(): kt = jnp.swapaxes(keys.reshape(blocks, BLK, width), 1, 2)  1.79 us

profile of v4, /device:TPU:27, one launch (start us, length us, event | category | flops | bytes accessed | tf_op | source)
XLA Modules:
  0.0 77.4 jit_solution(10293673023400317371)
XLA Ops:
  0.0 1.8 %copy.6 = bf16[8,128,128]{1,2,0:T(8,128)(2,1)} copy(bf16[8,128,128]{2,1,0:T(8,128)(2,1)} %bitcast.5) | data formatting | bytes 524288 | tf_op jit(solution)/shard_map/reshape | solution.py:440
  1.8 72.4 %shard_map.55 = bf16[256,4096]{1,0:T(8,128)(2,1)} custom-call(s32[8,8]{1,0:T(8,128)} %slash_ref.1, s32[8,8]{1,0:T(8,128)} %vertical_ref.1, bf16[1024,1024]{1,0:T(8,128)(2,1)} %queries_ref.1, bf16[8,128,128]{2,1,0:T(8,128)(2,1)} %bitcast.3, bf16[8,128,128]{2,1,0:T(8,128)(2,1)} %bitcast.4), custom_call_target="tpu_custom_call" | custom-call | tf_op jit(solution)/shard_map/pallas_call | solution.py:447
  74.2 3.1 %copy.8 = bf16[256,4096]{1,0:T(8,128)(2,1)} copy(bf16[256,4096]{1,0:T(8,128)(2,1)} %shard_map.55) | data formatting | bytes 4194304

commit v5 on v4

--- a/solution.py
+++ b/solution.py
@@ -253,24 +253,21 @@
             )
         return carry
 
-    def list_blocks(step, carry):
-        head, own = step // blocks, base + step % blocks
+    def list_block(head, own, row):
         reached = [own - slash_ref[head, n] for n in range(slashes)]
         for n, block in enumerate(reached):
             ok = block >= 0
-            index_ref[step * listed + n] = jnp.where(ok, block, own)
-            bias_ref[step * listed + n] = jnp.where(ok, 0.0, NEG)
+            index_ref[row + n] = jnp.where(ok, block, own)
+            bias_ref[row + n] = jnp.where(ok, 0.0, NEG)
         for n in range(verticals):
             block = vertical_ref[head, n]
             ok = block < own
             for other in reached:
                 ok = ok & (block != other)
             found = found_ref[head * verticals + n]
-            index_ref[step * listed + slashes + n] = jnp.where(ok, found, own)
-            bias_ref[step * listed + slashes + n] = jnp.where(ok, 0.0, NEG)
-        return carry
-
-    lists = heads * blocks
+            index_ref[row + slashes + n] = jnp.where(ok, found, own)
+            bias_ref[row + slashes + n] = jnp.where(ok, 0.0, NEG)
+
     loads[0].wait()
     for c in range(PIECES):
         pass_on(0, 0, c)
@@ -286,14 +283,9 @@
             pass_on(t, 0, c)
         if t == 1:
             lax.fori_loop(0, heads, place_verticals, 0)
-            lax.fori_loop(0, lists // 4, list_blocks, 0)
-        if t == 2:
-            lax.fori_loop(lists // 4, lists // 2, list_blocks, 0)
     loads[1].wait()
     for c in range(PIECES):
         pass_on(0, 1, c)
-    lax.fori_loop(lists // 2, lists, list_blocks, 0)
-    wait_cross(0)
     loads[2].wait()
 
     factor = math.log2(math.e) / math.sqrt(width)
@@ -346,6 +338,13 @@
             rows = pl.ds(pl.multiple_of(i * BLK, BLK), BLK)
             yield head, rows, columns, base + i, (head * blocks + i) * listed
 
+    def list_share(step):
+        for head, rows, columns, own, row in owned_blocks(step):
+            list_block(head, own, row)
+
+    def list_next(step):
+        list_share(jnp.minimum(step + 1, heads * groups - 1))
+
     def send_share(step):
         head, r = step // groups, step % groups
 
@@ -365,6 +364,7 @@
                 for t, c in due:
                     pass_on(t, 1, c)
 
+        list_next(step)
         for head, rows, columns, own, row in owned_blocks(step):
             rounded, total = block_weights(
                 q_ref[rows, columns], own, row, index_ref, bias_ref, kt_buf, causal, listed, factor
@@ -386,6 +386,7 @@
         return carry
 
     def one_share(step, carry):
+        list_next(step)
         for head, rows, columns, own, row in owned_blocks(step):
             rounded, total = block_weights(
                 q_ref[rows, columns], own, row, index_ref, bias_ref, kt_buf, causal, listed, factor
@@ -399,6 +400,8 @@
         send_share(step)
         return carry
 
+    list_share(jnp.int32(0))
+    wait_cross(0)
     lax.fori_loop(0, early * groups, weigh_early, 0)
     wait_cross(1)
     lax.fori_loop(0, early * groups, mix_early, 0)

time: 78.2 us -> 84.1 us (1.075)
  Pallas kernels: 72.4 us -> 78.4 us
    pallas_call x1, Pallas kernels: 72.4 us -> 78.4 us  [shards(): pl.pallas_call(functools.partial(layer_kernel, blocks=blocks, listed=list...]
where the time goes in v5:
time: 84.1 us; the launch traced here: 83.3 us
  Pallas kernels  78.4 us (93%)
  local copies, waits for them, and re-layouts  4.92 us (6%)
    pallas_call x1, Pallas kernels, shards(): pl.pallas_call(functools.partial(layer_kernel, blocks=blocks, listed=list...  78.4 us
    unnamed x1, local copies, waits for them, and re-layouts  3.13 us
    reshape x1, local copies, waits for them, and re-layouts, shards(): kt = jnp.swapaxes(keys.reshape(blocks, BLK, width), 1, 2)  1.79 us

profile of v5, /device:TPU:27, one launch (start us, length us, event | category | flops | bytes accessed | tf_op | source)
XLA Modules:
  0.0 83.3 jit_solution(8083330564221302580)
XLA Ops:
  0.0 1.8 %copy.6 = bf16[8,128,128]{1,2,0:T(8,128)(2,1)} copy(bf16[8,128,128]{2,1,0:T(8,128)(2,1)} %bitcast.5) | data formatting | bytes 524288 | tf_op jit(solution)/shard_map/reshape | solution.py:443
  1.8 78.4 %shard_map.55 = bf16[256,4096]{1,0:T(8,128)(2,1)} custom-call(s32[8,8]{1,0:T(8,128)} %slash_ref.1, s32[8,8]{1,0:T(8,128)} %vertical_ref.1, bf16[1024,1024]{1,0:T(8,128)(2,1)} %queries_ref.1, bf16[8,128,128]{2,1,0:T(8,128)(2,1)} %bitcast.3, bf16[8,128,128]{2,1,0:T(8,128)(2,1)} %bitcast.4), custom_call_target="tpu_custom_call" | custom-call | tf_op jit(solution)/shard_map/pallas_call | solution.py:450
  80.2 3.1 %copy.8 = bf16[256,4096]{1,0:T(8,128)(2,1)} copy(bf16[256,4096]{1,0:T(8,128)(2,1)} %shard_map.55) | data formatting | bytes 4194304
